TPU v7x, 32 devices: a whole 2x2x4 slice. The times are simulated.
32 devices in a mesh: expert: 2 (over x), batch: 4 (over z), seq: 4 (over y, core).
Axes of the slice: x: 2, y: 2, z: 4, core: 2. Of those that a mesh axis runs over, the one named last changes fastest.
Arguments:
- queries: bfloat16 [2, 4, 2, 384, 4096], P('expert', 'batch', None, 'seq'), may hold values from -36 to 36
- keys: bfloat16 [2, 4, 2, 384, 4096], P('expert', 'batch', None, 'seq'), may hold values from -21 to 21
- values: bfloat16 [2, 4, 2, 384, 4096], P('expert', 'batch', None, 'seq'), may hold values from -6 to 6
- latents: bfloat16 [2, 4, 384, 4096], P('expert', 'batch', 'seq'), may hold values from -6 to 6
- gain: bfloat16 [2, 4096], P('expert'), may hold values from 0.099609375 to 1.8984375
- steps_table: int32 [2, 4], P('expert', 'batch'), may hold values from 0 to 38
- flags: int32 [4], P('batch'), may hold values 0 or 1
Outputs:
- denoised: bfloat16 [2, 4, 384, 4096], P('expert', 'batch', 'seq')
- next_latents: bfloat16 [2, 4, 384, 4096], P('expert', 'batch', 'seq')
All inputs are finite; a program needn't handle non-finite values. No bound on the sum of `flags` on one device may be relied on, other than what follows from the above.
Results may differ from a plain program's by a relative error of at most 0.006.
Values may be sent and summed in bfloat16 or wider, within the bound.
A program may use at most 64 MiB of HBM per device.

v0:
```python
import functools

import jax
import jax.numpy as jnp
from jax import lax
from jax.experimental import pallas as pl
from jax.experimental.pallas import tpu as pltpu
from jax.sharding import PartitionSpec as P

HDIM = 128
STEPS = 40


GUIDANCE = 3.5
flow_shift = 5.0


def from_partner(block, axis, bit):
    count = lax.axis_size(axis)
    route = []
    for low in range(count):
        high = low | 1 << bit
        if high != low and high < count:
            route += [(low, high), (high, low)]
    return lax.ppermute(block, axis, route)


def sigma_of(step):
    level = 1.0 - step.astype(jnp.float32) / STEPS
    return flow_shift * level / (1.0 + (flow_shift - 1.0) * level)


def combine(cond, uncond):
    base = uncond.astype(jnp.float32)
    return (base + GUIDANCE * (cond.astype(jnp.float32) - base)).astype(jnp.bfloat16)


def attend(stacked):
    query_heads, key_heads, value_heads = stacked
    items, length, width_dev = query_heads.shape
    heads_dev = width_dev // HDIM
    block = 512 if length % 512 == 0 else length
    key_rows = key_heads.reshape(items, length, heads_dev, HDIM)
    value_rows = value_heads.reshape(items, length, heads_dev, HDIM)
    query_blocks = query_heads.reshape(items, length // block, block, heads_dev, HDIM).transpose(
        1, 0, 2, 3, 4
    )

    def one_block(query_part):
        scores = jnp.einsum(
            "nqhd,nkhd->nhqk", query_part, key_rows, preferred_element_type=jnp.float32
        ) * HDIM ** (-0.5)
        weights = jax.nn.softmax(scores, axis=-1).astype(jnp.bfloat16)
        return jnp.einsum(
            "nhqk,nkhd->nqhd", weights, value_rows, preferred_element_type=jnp.float32
        ).astype(jnp.bfloat16)

    result = lax.map(one_block, query_blocks)
    return result.transpose(1, 0, 2, 3, 4).reshape(items, length, width_dev)


def exchange_heads(queries, keys, values, latents, gain, steps_table, flags):
    attended = attend(
        (
            lax.all_to_all(queries[0, 0], "seq", split_axis=2, concat_axis=1, tiled=True),
            lax.all_to_all(keys[0, 0], "seq", split_axis=2, concat_axis=1, tiled=True),
            lax.all_to_all(values[0, 0], "seq", split_axis=2, concat_axis=1, tiled=True),
        )
    )
    guided = lax.all_to_all(
        combine(attended[0], attended[1]), "seq", split_axis=0, concat_axis=1, tiled=True
    )
    guided_f32 = guided.astype(jnp.float32)
    scale = lax.rsqrt(jnp.mean(guided_f32 * guided_f32, axis=-1, keepdims=True) + 1e-06)
    velocity = guided_f32 * scale * gain[0].astype(jnp.float32)[None, :]
    step_now = steps_table[0, 0]
    sigma_now = sigma_of(step_now)
    sigma_next = sigma_of(step_now + 1)
    current = latents[0, 0].astype(jnp.float32)
    denoised = (current - sigma_now * velocity).astype(jnp.bfloat16)
    moved = (current + (sigma_next - sigma_now) * velocity).astype(jnp.bfloat16)
    partner = from_partner(moved, "expert", 0)
    next_latents = jnp.where(flags[0] == 1, partner, moved)
    return (denoised[None, None], next_latents[None, None])


MESH = pl.DeviceIdType.MESH
HEADS_AT_ONCE = 4
PIECE = 16
LATE = 2


def head_cols(head):
    return pl.ds(pl.multiple_of(head * HDIM, HDIM), HDIM)


def partial_attention(query, key_rows, value_rows):
    scores = lax.dot_general(
        query, key_rows, (((1,), (1,)), ((), ())), preferred_element_type=jnp.float32
    )
    top = jnp.max(scores, axis=-1, keepdims=True)
    powers = jnp.exp((scores - top) * HDIM ** (-0.5))
    total = jnp.sum(powers, axis=-1, keepdims=True)
    part = jnp.dot(powers.astype(jnp.bfloat16), value_rows, preferred_element_type=jnp.float32)
    return part / total, top * HDIM ** (-0.5) + jnp.log(total)


def share(mine, other):
    return 1.0 / (1.0 + jnp.exp(other - mine))


def pair_kernel(
    queries, keys, values, latents, gain, steps,
    denoised, moved, partner,
    q_own, q_far, k_all, v_all, part_own, part_far, part_back, current, den_rows, mov_rows,
    guided, lse_own, lse_peer, lse_far, lse_back, gain_now, gain_move,
    load_sems, kv_sems, q_sems, lse_sems, back_sems, back_lse_sems, cross_sems, store_sems,
):
    seq = lax.axis_index("seq")
    size = lax.axis_size("seq")
    beside = {"seq": seq + 1 - 2 * lax.rem(seq, 2)}
    across = {"seq": lax.rem(seq + size // 2, size)}
    other = {"expert": 1 - lax.axis_index("expert")}
    branches, rows, width = queries.shape
    heads = width // HDIM
    half = rows // 2
    pieces = rows // PIECE

    own_keys = pl.ds(0, rows)
    loads = [
        pltpu.make_async_copy(queries, q_own, load_sems.at[0]),
        pltpu.make_async_copy(keys, k_all.at[:, own_keys], load_sems.at[1]),
        pltpu.make_async_copy(values, v_all.at[:, own_keys], load_sems.at[2]),
        pltpu.make_async_copy(latents, current, load_sems.at[3]),
    ]
    for load in loads:
        load.start()

    barrier = pltpu.get_barrier_semaphore()
    for peer in (beside, across, other):
        pl.semaphore_signal(barrier, inc=1, device_id=peer, device_id_type=MESH)
    pl.semaphore_wait(barrier, 3)

    def remote(source, target, sems, index, peer):
        return pltpu.make_async_remote_copy(
            src_ref=source, dst_ref=target, send_sem=sems.at[0, index],
            recv_sem=sems.at[1, index], device_id=peer, device_id_type=MESH,
        )

    q_sends = [
        remote(queries.at[:, pl.ds(at * PIECE, PIECE)], q_far.at[:, pl.ds(at * PIECE, PIECE)],
               q_sems, at, across)
        for at in range(pieces)
    ]
    peer_keys = pl.ds(rows, rows)
    kv_sends = [
        remote(keys, k_all.at[:, peer_keys], kv_sems, 0, beside),
        remote(values, v_all.at[:, peer_keys], kv_sems, 1, beside),
    ]
    for send in kv_sends:
        send.start()
    for send in q_sends[:-LATE]:
        send.start()

    step = jnp.full((1, HDIM), steps[0, 0], jnp.int32)
    sigma_now = sigma_of(step)[:, :1]
    sigma_next = sigma_of(step + 1)[:, :1]
    row = gain[...].astype(jnp.float32)
    gain_now[...] = sigma_now * row
    gain_move[...] = (sigma_next - sigma_now) * row

    for load in loads:
        load.wait()
    for send in kv_sends:
        send.wait_recv()

    lane = lax.broadcasted_iota(jnp.int32, (1, HDIM), 1)

    def own_heads(step_at, lse):
        for extra in range(HEADS_AT_ONCE):
            head = step_at * HEADS_AT_ONCE + extra
            cols = head_cols(head)
            for branch in range(branches):
                part, stat = partial_attention(
                    q_own[branch, :, cols], k_all[branch, :, cols], v_all[branch, :, cols]
                )
                part_own[branch, :, cols] = part
                lse = jnp.where(lane == branch * heads + head, stat, lse)
        return lse

    lse_own[...] = lax.fori_loop(
        0, heads // HEADS_AT_ONCE, own_heads, jnp.zeros((rows, HDIM), jnp.float32)
    )
    lse_send = remote(lse_own, lse_peer, lse_sems, 0, across)
    lse_send.start()
    for send in q_sends[-LATE:]:
        send.start()
    lse_send.wait_recv()

    def back_copies(piece):
        at = pl.ds(pl.multiple_of(piece * PIECE, PIECE), PIECE)
        return (
            remote(lse_far.at[at], lse_back.at[at], back_lse_sems, piece, across),
            remote(part_far.at[at], part_back.at[at], back_sems, piece, across),
        )

    for at in range(2):
        for send in q_sends[at * pieces // 2 : (at + 1) * pieces // 2]:
            send.wait_recv()
        here = pl.ds(at * half, half)
        peer_lse = lse_peer[here, :]

        def far_heads(step_at, lse):
            for extra in range(HEADS_AT_ONCE):
                head = step_at * HEADS_AT_ONCE + extra
                cols = head_cols(head)
                terms = []
                for branch in range(branches):
                    part, stat = partial_attention(
                        q_far[branch, here, cols], k_all[branch, :, cols], v_all[branch, :, cols]
                    )
                    spot = lane == branch * heads + head
                    lse = jnp.where(spot, stat, lse)
                    theirs = jnp.sum(jnp.where(spot, peer_lse, 0.0), axis=-1, keepdims=True)
                    terms.append(part * share(stat, theirs))
                part_far[here, cols] = (GUIDANCE * terms[0] + (1.0 - GUIDANCE) * terms[1]).astype(
                    jnp.bfloat16
                )
            return lse

        lse_far[here, :] = lax.fori_loop(
            0, heads // HEADS_AT_ONCE, far_heads, jnp.zeros((half, HDIM), jnp.float32)
        )
        for piece in range(at * pieces // 2, (at + 1) * pieces // 2):
            for copy in back_copies(piece):
                copy.start()

    def result_copies(piece):
        at = pl.ds(pl.multiple_of(piece * PIECE, PIECE), PIECE)
        return (
            remote(mov_rows.at[at], partner.at[at], cross_sems, piece, other),
            pltpu.make_async_copy(den_rows.at[at], denoised.at[at], store_sems.at[0, piece]),
            pltpu.make_async_copy(mov_rows.at[at], moved.at[at], store_sems.at[1, piece]),
        )

    def finish(piece, carry):
        at = pl.ds(pl.multiple_of(piece * PIECE, PIECE), PIECE)
        for copy in back_copies(piece):
            copy.wait_recv()
        weight = share(lse_own[at, :], lse_back[at, :])
        squares = jnp.zeros((PIECE, HDIM), jnp.float32)
        for head in range(heads):
            cols = pl.ds(head * HDIM, HDIM)
            uncond = heads + head
            value = (
                GUIDANCE * weight[:, head : head + 1] * part_own[0, at, cols]
                + (1.0 - GUIDANCE) * weight[:, uncond : uncond + 1] * part_own[1, at, cols]
                + part_back[at, cols].astype(jnp.float32)
            ).astype(jnp.bfloat16).astype(jnp.float32)
            guided[:, cols] = value
            squares += value * value
        mean = jnp.sum(squares, axis=-1, keepdims=True) / width
        scale = lax.rsqrt(mean + 1e-06)
        for head in range(heads):
            cols = pl.ds(head * HDIM, HDIM)
            unit = guided[:, cols] * scale
            now = current[at, cols].astype(jnp.float32)
            mov_rows[at, cols] = (now + gain_move[:, cols] * unit).astype(jnp.bfloat16)
            den_rows[at, cols] = (now - gain_now[:, cols] * unit).astype(jnp.bfloat16)
        for copy in result_copies(piece):
            copy.start()
        return carry

    lax.fori_loop(0, pieces, finish, 0)

    for send in q_sends + kv_sends + [lse_send]:
        send.wait_send()

    def drain(piece, carry):
        for copy in back_copies(piece):
            copy.wait_send()
        for copy in result_copies(piece):
            copy.wait()
        return carry

    lax.fori_loop(0, pieces, drain, 0)


def exchange_queries(queries, keys, values, latents, gain, steps_table, flags):
    branches, rows, width = queries.shape[2:]
    pieces = rows // PIECE
    whole = jax.ShapeDtypeStruct((rows, width), jnp.bfloat16)
    hbm = pl.BlockSpec(memory_space=pltpu.HBM)
    low = functools.partial(pltpu.VMEM, dtype=jnp.bfloat16)
    high = functools.partial(pltpu.VMEM, dtype=jnp.float32)
    dma = pltpu.SemaphoreType.DMA
    denoised, moved, partner = pl.pallas_call(
        pair_kernel,
        out_shape=(whole, whole, whole),
        in_specs=[hbm] * 4
        + [pl.BlockSpec(memory_space=pltpu.VMEM), pl.BlockSpec(memory_space=pltpu.SMEM)],
        out_specs=(hbm, hbm, hbm),
        scratch_shapes=[
            low((branches, rows, width)),
            low((branches, rows, width)),
            low((branches, 2 * rows, width)),
            low((branches, 2 * rows, width)),
            high((branches, rows, width)),
            low((rows, width)),
            low((rows, width)),
            low((rows, width)),
            low((rows, width)),
            low((rows, width)),
            high((PIECE, width)),
            high((rows, HDIM)),
            high((rows, HDIM)),
            high((rows, HDIM)),
            high((rows, HDIM)),
            high((1, width)),
            high((1, width)),
            dma((4,)),
            dma((2, 2)),
            dma((2, pieces)),
            dma((2, 1)),
            dma((2, pieces)),
            dma((2, pieces)),
            dma((2, pieces)),
            dma((2, pieces)),
        ],
        compiler_params=pltpu.CompilerParams(collective_id=0, has_side_effects=True),
    )(queries[0, 0], keys[0, 0], values[0, 0], latents[0, 0], gain, steps_table)
    next_latents = jnp.where(flags[0] == 1, partner, moved)
    return (denoised[None, None], next_latents[None, None])


def per_device(*blocks):
    branches, rows, width = blocks[0].shape[2:]
    paired = (
        lax.axis_size("seq") == 2 * 2
        and lax.axis_size("expert") == 2
        and rows % (2 * PIECE) == 0
        and branches * width // HDIM <= HDIM
    )
    return (exchange_queries if paired else exchange_heads)(*blocks)


def solution(mesh):
    placed = (
        P("expert", "batch", None, "seq", None),
        P("expert", "batch", None, "seq", None),
        P("expert", "batch", None, "seq", None),
        P("expert", "batch", "seq", None),
        P("expert", None),
        P("expert", "batch"),
        P("batch"),
    )
    return jax.shard_map(
        per_device,
        mesh=mesh,
        in_specs=placed,
        out_specs=(P("expert", "batch", "seq", None), P("expert", "batch", "seq", None)),
        check_vma=False,
    )
```

profile of v0, /device:TPU:0, one launch (start us, length us, event | category | flops | bytes accessed | tf_op | source)
XLA Modules:
  0.0 89.5 jit_solution(9070299570204854354)
XLA Ops:
  1.9 84.5 %shard_map.86 = (bf16[96,4096]{1,0:T(8,128)(2,1)}, bf16[96,4096]{1,0:T(8,128)(2,1)}, bf16[96,4096]{1,0:T(8,128)(2,1)}) custom-call(bf16[2,96,4096]{2,1,0:T(8,128)(2,1)} %bitcast.8, bf16[2,96,4096]{2,1,0:T(8,128)(2,1)} %bitcast.9, bf16[2,96,4096]{2,1,0:T(8,128)(2,1)} %bitcast.10, bf16[96,4096]{1,0:T(8,128)(2,1)} %bitcast.12, bf16[1,4096]{1,0:T(2,128)(2,1)} %gain.1, ...), custom_call_target="tpu_custom_call" | custom-call | tf_op jit(solution)/shard_map/pallas_call | solution.py:297
  86.5 0.0 copy-start
  86.5 2.2 %select_bitcast_fusion = bf16[1,1,96,4096]{3,2,1,0:T(8,128)(2,1)} fusion(bf16[96,4096]{1,0:T(8,128)(2,1)} %get-tuple-element.6, bf16[96,4096]{1,0:T(8,128)(2,1)} %get-tuple-element.7, pred[]{:T(512)} %bitcast.5), kind=kLoop, calls=%fused_computation | loop fusion | flops 393216 | bytes 2359297 | tf_op jit(solution)/shard_map/broadcast_in_dim | solution.py:333
  88.7 0.0 copy-done
  88.7 0.9 copy.12
Async XLA Ops:
  86.5 2.2 %copy-start = (bf16[96,4096]{1,0:T(8,128)(2,1)S(1)}, bf16[96,4096]{1,0:T(8,128)(2,1)}, u32[]{:S(2)}) copy-start(bf16[96,4096]{1,0:T(8,128)(2,1)} %get-tuple-element.5) | copy-start | bytes 2359300
where the time goes:
time: 89.8 us; the launch traced here: 89.5 us
  Pallas kernels  84.5 us (94%)
  other arithmetic  2.18 us (2%)
  between operations  1.94 us (2%)
    pallas_call x1, Pallas kernels, exchange_queries(): pl.pallas_call(pair_kernel, out_shape=(whole, whole, whole), in_specs=[hb...  84.5 us
    broadcast_in_dim x1, other arithmetic, exchange_queries(): return (denoised[None, None], next_latents[None, None])  2.18 us

commit v1 on v0

v1 whole, which is shorter than its diff:
```python
import functools

import jax
import jax.numpy as jnp
from jax import lax
from jax.experimental import pallas as pl
from jax.experimental.pallas import tpu as pltpu
from jax.sharding import PartitionSpec as P

HDIM = 128
STEPS = 40


GUIDANCE = 3.5
flow_shift = 5.0


def from_partner(block, axis, bit):
    count = lax.axis_size(axis)
    route = []
    for low in range(count):
        high = low | 1 << bit
        if high != low and high < count:
            route += [(low, high), (high, low)]
    return lax.ppermute(block, axis, route)


def sigma_of(step):
    level = 1.0 - step.astype(jnp.float32) / STEPS
    return flow_shift * level / (1.0 + (flow_shift - 1.0) * level)


def combine(cond, uncond):
    base = uncond.astype(jnp.float32)
    return (base + GUIDANCE * (cond.astype(jnp.float32) - base)).astype(jnp.bfloat16)


def attend(stacked):
    query_heads, key_heads, value_heads = stacked
    items, length, width_dev = query_heads.shape
    heads_dev = width_dev // HDIM
    block = 512 if length % 512 == 0 else length
    key_rows = key_heads.reshape(items, length, heads_dev, HDIM)
    value_rows = value_heads.reshape(items, length, heads_dev, HDIM)
    query_blocks = query_heads.reshape(items, length // block, block, heads_dev, HDIM).transpose(
        1, 0, 2, 3, 4
    )

    def one_block(query_part):
        scores = jnp.einsum(
            "nqhd,nkhd->nhqk", query_part, key_rows, preferred_element_type=jnp.float32
        ) * HDIM ** (-0.5)
        weights = jax.nn.softmax(scores, axis=-1).astype(jnp.bfloat16)
        return jnp.einsum(
            "nhqk,nkhd->nqhd", weights, value_rows, preferred_element_type=jnp.float32
        ).astype(jnp.bfloat16)

    result = lax.map(one_block, query_blocks)
    return result.transpose(1, 0, 2, 3, 4).reshape(items, length, width_dev)


def exchange_heads(queries, keys, values, latents, gain, steps_table, flags):
    attended = attend(
        (
            lax.all_to_all(queries[0, 0], "seq", split_axis=2, concat_axis=1, tiled=True),
            lax.all_to_all(keys[0, 0], "seq", split_axis=2, concat_axis=1, tiled=True),
            lax.all_to_all(values[0, 0], "seq", split_axis=2, concat_axis=1, tiled=True),
        )
    )
    guided = lax.all_to_all(
        combine(attended[0], attended[1]), "seq", split_axis=0, concat_axis=1, tiled=True
    )
    guided_f32 = guided.astype(jnp.float32)
    scale = lax.rsqrt(jnp.mean(guided_f32 * guided_f32, axis=-1, keepdims=True) + 1e-06)
    velocity = guided_f32 * scale * gain[0].astype(jnp.float32)[None, :]
    step_now = steps_table[0, 0]
    sigma_now = sigma_of(step_now)
    sigma_next = sigma_of(step_now + 1)
    current = latents[0, 0].astype(jnp.float32)
    denoised = (current - sigma_now * velocity).astype(jnp.bfloat16)
    moved = (current + (sigma_next - sigma_now) * velocity).astype(jnp.bfloat16)
    partner = from_partner(moved, "expert", 0)
    next_latents = jnp.where(flags[0] == 1, partner, moved)
    return (denoised[None, None], next_latents[None, None])


MESH = pl.DeviceIdType.MESH
HEADS_AT_ONCE = 4
EARLY = 3
TILE = 8
LOG2E = 1.4426950408889634


def partial_attention(query, key_rows, value_rows):
    scores = lax.dot_general(
        query, key_rows, (((1,), (1,)), ((), ())), preferred_element_type=jnp.float32
    )
    top = jnp.max(scores, axis=-1, keepdims=True)
    powers = jnp.exp2((scores - top) * (HDIM ** (-0.5) * LOG2E))
    total = jnp.sum(powers, axis=-1, keepdims=True)
    part = jnp.dot(powers.astype(jnp.bfloat16), value_rows, preferred_element_type=jnp.float32)
    return part, total, top * (HDIM ** (-0.5) * LOG2E) + jnp.log2(total)


def share(mine, other):
    return 1.0 / (1.0 + jnp.exp2(other - mine))


def pack(stat, spot, packed):
    lane = lax.broadcasted_iota(jnp.int32, packed.shape, 1)
    for at in range(stat.shape[0] // TILE):
        here = stat[at * TILE : (at + 1) * TILE]
        packed = jnp.where(lane == at * TILE + spot, here, packed)
    return packed


def unpack(packed, spot, rows):
    return jnp.concatenate(
        [packed[:, at * TILE + spot : at * TILE + spot + 1] for at in range(rows // TILE)], axis=0
    )


def pair_kernel(
    queries, keys, values, latents, gain, steps, flags,
    denoised, next_latents,
    q_own, q_far, k_all, v_all, part_own, part_far, part_back, guided, guided_peer,
    now, now_peer, lse_own, lse_peer, lse_far, lse_back, squares, squares_peer,
    gain_now, gain_move, gain_peer,
    load_sems, kv_sems, q_sems, lse_sems, back_sems, stat_sems, cross_sems, ahead_sems,
):
    seq = lax.axis_index("seq")
    size = lax.axis_size("seq")
    beside = {"seq": seq + 1 - 2 * lax.rem(seq, 2)}
    across = {"seq": lax.rem(seq + size // 2, size)}
    other = {"expert": 1 - lax.axis_index("expert")}
    branches, rows, width = queries.shape
    group = HEADS_AT_ONCE * HDIM
    groups = width // group

    own_keys = pl.ds(0, rows)
    peer_keys = pl.ds(rows, rows)
    loads = [
        pltpu.make_async_copy(keys, k_all.at[:, own_keys], load_sems.at[0]),
        pltpu.make_async_copy(queries, q_own, load_sems.at[1]),
        pltpu.make_async_copy(values, v_all.at[:, own_keys], load_sems.at[2]),
        pltpu.make_async_copy(latents, now, load_sems.at[3]),
    ]
    for load in loads:
        load.start()

    barrier = pltpu.get_barrier_semaphore()
    for peer in (beside, across, other):
        pl.semaphore_signal(barrier, inc=1, device_id=peer, device_id_type=MESH)
    pl.semaphore_wait(barrier, 3)

    def remote(source, target, sems, index, peer):
        return pltpu.make_async_remote_copy(
            src_ref=source, dst_ref=target, send_sem=sems.at[0, index],
            recv_sem=sems.at[1, index], device_id=peer, device_id_type=MESH,
        )

    def span(at):
        return pl.ds(pl.multiple_of(at * group, group), group)

    def head_span(at, extra):
        return pl.ds(pl.multiple_of(at * group + extra * HDIM, HDIM), HDIM)

    def q_send(at):
        cols = span(at)
        return remote(queries.at[:, :, cols], q_far.at[:, :, cols], q_sems, at, across)

    def kv_sends(at):
        cols = span(at)
        return (
            remote(keys.at[:, :, cols], k_all.at[:, peer_keys, cols], kv_sems, 2 * at, beside),
            remote(values.at[:, :, cols], v_all.at[:, peer_keys, cols], kv_sems, 2 * at + 1, beside),
        )

    def lse_send(at):
        return remote(lse_own.at[at], lse_peer.at[at], lse_sems, at, across)

    def back_sends(at):
        cols = span(at)
        return (
            remote(lse_far.at[at], lse_back.at[at], stat_sems, at, across),
            remote(part_far.at[:, cols], part_back.at[:, cols], back_sems, at, across),
        )

    def cross_send(at):
        cols = span(at)
        return remote(guided.at[:, cols], guided_peer.at[:, cols], cross_sems, at, other)

    for at in range(min(EARLY, groups)):
        q_send(at).start()

    def start_kv(at, carry):
        for send in kv_sends(at):
            send.start()
        return carry

    lax.fori_loop(0, groups, start_kv, 0)
    ahead = [
        remote(latents, now_peer, ahead_sems, 0, other),
        remote(gain_move, gain_peer, ahead_sems, 1, other),
    ]
    ahead[0].start()

    step = jnp.full((1, HDIM), steps[0, 0], jnp.int32)
    sigma_now = sigma_of(step)[:, :1]
    sigma_next = sigma_of(step + 1)[:, :1]
    row = gain[...].astype(jnp.float32)
    gain_now[...] = sigma_now * row
    gain_move[...] = (sigma_next - sigma_now) * row
    squares[...] = jnp.zeros_like(squares)
    squares_peer[...] = jnp.zeros_like(squares_peer)

    for load in loads:
        load.wait()

    def own_group(at, carry):
        for send in kv_sends(at):
            send.wait_recv()
        lse = jnp.zeros((TILE, HDIM), jnp.float32)
        for extra in range(HEADS_AT_ONCE):
            cols = head_span(at, extra)
            for branch in range(branches):
                part, total, stat = partial_attention(
                    q_own[branch, :, cols], k_all[branch, :, cols], v_all[branch, :, cols]
                )
                part_own[branch, :, cols] = part / total
                lse = pack(stat, extra * branches + branch, lse)
        lse_own[at] = lse
        lse_send(at).start()

        @pl.when(at + EARLY < groups)
        def _():
            q_send(at + EARLY).start()

        return carry

    lax.fori_loop(0, groups, own_group, 0)
    ahead[1].start()

    def far_group(at, carry):
        lse_send(at).wait_recv()
        q_send(at).wait_recv()
        theirs = lse_peer[at]
        lse = jnp.zeros((TILE, HDIM), jnp.float32)
        for extra in range(HEADS_AT_ONCE):
            cols = head_span(at, extra)
            terms = []
            for branch, factor in ((0, GUIDANCE), (1, 1.0 - GUIDANCE)):
                part, total, stat = partial_attention(
                    q_far[branch, :, cols], k_all[branch, :, cols], v_all[branch, :, cols]
                )
                spot = extra * branches + branch
                lse = pack(stat, spot, lse)
                terms.append(part * (factor * share(stat, unpack(theirs, spot, rows)) / total))
            part_far[:, cols] = (terms[0] + terms[1]).astype(jnp.bfloat16)
        lse_far[at] = lse
        for send in back_sends(at):
            send.start()
        return carry

    lax.fori_loop(0, groups, far_group, 0)

    def add_squares(target, values_here):
        target[...] += values_here * values_here

    def finish_group(at, carry):
        for send in back_sends(at):
            send.wait_recv()
        weight = share(lse_own[at], lse_back[at])
        for extra in range(HEADS_AT_ONCE):
            cols = head_span(at, extra)
            spot = extra * branches
            value = (
                GUIDANCE * unpack(weight, spot, rows) * part_own[0, :, cols]
                + (1.0 - GUIDANCE) * unpack(weight, spot + 1, rows) * part_own[1, :, cols]
                + part_back[:, cols].astype(jnp.float32)
            ).astype(jnp.bfloat16)
            guided[:, cols] = value
            add_squares(squares, value.astype(jnp.float32))
        cross_send(at).start()
        return carry

    lax.fori_loop(0, groups, finish_group, 0)

    scale = lax.rsqrt(jnp.sum(squares[...], axis=-1, keepdims=True) / width + 1e-06)

    def denoise_group(at, carry):
        for extra in range(HEADS_AT_ONCE):
            cols = head_span(at, extra)
            unit = guided[:, cols].astype(jnp.float32) * scale
            denoised[:, cols] = (
                now[:, cols].astype(jnp.float32) - gain_now[:, cols] * unit
            ).astype(jnp.bfloat16)
        return carry

    lax.fori_loop(0, groups, denoise_group, 0)

    def peer_squares(at, carry):
        cross_send(at).wait_recv()
        for extra in range(HEADS_AT_ONCE):
            add_squares(squares_peer, guided_peer[:, head_span(at, extra)].astype(jnp.float32))
        return carry

    lax.fori_loop(0, groups, peer_squares, 0)
    for send in ahead:
        send.wait_recv()
    scale_peer = lax.rsqrt(jnp.sum(squares_peer[...], axis=-1, keepdims=True) / width + 1e-06)
    trade = jnp.full((rows, HDIM), flags[0], jnp.int32) == 1

    def move_group(at, carry):
        for extra in range(HEADS_AT_ONCE):
            cols = head_span(at, extra)
            mine = now[:, cols].astype(jnp.float32) + gain_move[:, cols] * (
                guided[:, cols].astype(jnp.float32) * scale
            )
            theirs = now_peer[:, cols].astype(jnp.float32) + gain_peer[:, cols] * (
                guided_peer[:, cols].astype(jnp.float32) * scale_peer
            )
            next_latents[:, cols] = jnp.where(trade, theirs, mine).astype(jnp.bfloat16)
        return carry

    lax.fori_loop(0, groups, move_group, 0)

    def drain(at, carry):
        for send in (q_send(at), lse_send(at), cross_send(at)) + kv_sends(at) + back_sends(at):
            send.wait_send()
        return carry

    lax.fori_loop(0, groups, drain, 0)
    for send in ahead:
        send.wait_send()


def exchange_queries(queries, keys, values, latents, gain, steps_table, flags):
    branches, rows, width = queries.shape[2:]
    groups = width // (HEADS_AT_ONCE * HDIM)
    whole = jax.ShapeDtypeStruct((rows, width), jnp.bfloat16)
    hbm = pl.BlockSpec(memory_space=pltpu.HBM)
    vmem = pl.BlockSpec(memory_space=pltpu.VMEM)
    smem = pl.BlockSpec(memory_space=pltpu.SMEM)
    low = functools.partial(pltpu.VMEM, dtype=jnp.bfloat16)
    high = functools.partial(pltpu.VMEM, dtype=jnp.float32)
    dma = pltpu.SemaphoreType.DMA
    stats = high((groups, TILE, HDIM))
    denoised, next_latents = pl.pallas_call(
        pair_kernel,
        out_shape=(whole, whole),
        in_specs=[hbm] * 4 + [vmem, smem, smem],
        out_specs=(vmem, vmem),
        scratch_shapes=[
            low((branches, rows, width)),
            low((branches, rows, width)),
            low((branches, 2 * rows, width)),
            low((branches, 2 * rows, width)),
            high((branches, rows, width)),
            low((rows, width)),
            low((rows, width)),
            low((rows, width)),
            low((rows, width)),
            low((rows, width)),
            low((rows, width)),
            stats,
            stats,
            stats,
            stats,
            high((rows, HDIM)),
            high((rows, HDIM)),
            high((1, width)),
            high((1, width)),
            high((1, width)),
            dma((4,)),
            dma((2, 2 * groups)),
            dma((2, groups)),
            dma((2, groups)),
            dma((2, groups)),
            dma((2, groups)),
            dma((2, groups)),
            dma((2, 2)),
        ],
        compiler_params=pltpu.CompilerParams(collective_id=0, has_side_effects=True),
    )(queries[0, 0], keys[0, 0], values[0, 0], latents[0, 0], gain, steps_table, flags)
    return (denoised[None, None], next_latents[None, None])


def per_device(*blocks):
    branches, rows, width = blocks[0].shape[2:]
    paired = (
        lax.axis_size("seq") == 2 * 2
        and lax.axis_size("expert") == 2
        and branches == 2
        and rows % (2 * TILE) == 0
        and rows // TILE * HEADS_AT_ONCE * branches <= HDIM
        and HEADS_AT_ONCE * branches <= TILE
        and width % (HEADS_AT_ONCE * HDIM) == 0
    )
    return (exchange_queries if paired else exchange_heads)(*blocks)


def solution(mesh):
    placed = (
        P("expert", "batch", None, "seq", None),
        P("expert", "batch", None, "seq", None),
        P("expert", "batch", None, "seq", None),
        P("expert", "batch", "seq", None),
        P("expert", None),
        P("expert", "batch"),
        P("batch"),
    )
    return jax.shard_map(
        per_device,
        mesh=mesh,
        in_specs=placed,
        out_specs=(P("expert", "batch", "seq", None), P("expert", "batch", "seq", None)),
        check_vma=False,
    )
```

time: 89.8 us -> 75 us (0.84)
  Pallas kernels: 84.5 us -> 69.8 us
  other arithmetic: 2.18 us -> 0 us
  local copies, waits for them, and re-layouts: 0.88 us -> 3.02 us
    pallas_call x1, Pallas kernels: 84.5 us -> 69.8 us  [exchange_queries(): pl.pallas_call(pair_kernel, out_shape=(whole, whole), in_specs=[hbm] * 4...]
    broadcast_in_dim x1 -> x0, other arithmetic: 2.18 us -> none  [exchange_queries(): return (denoised[None, None], next_latents[None, None])]
    unnamed x3 -> x4, local copies, waits for them, and re-layouts: 0.88 us -> 3.02 us
where the time goes in v1:
time: 75 us; the launch traced here: 74.7 us
  Pallas kernels  69.8 us (93%)
  local copies, waits for them, and re-layouts  3.02 us (4%)
  between operations  1.94 us (3%)
    pallas_call x1, Pallas kernels, exchange_queries(): pl.pallas_call(pair_kernel, out_shape=(whole, whole), in_specs=[hbm] * 4...  69.8 us
    unnamed x4, local copies, waits for them, and re-layouts  3.02 us

profile of v1, /device:TPU:0, one launch (start us, length us, event | category | flops | bytes accessed | tf_op | source)
XLA Modules:
  0.0 74.7 jit_solution(11220341603595346933)
XLA Ops:
  1.9 69.8 %shard_map.86 = (bf16[96,4096]{1,0:T(8,128)(2,1)}, bf16[96,4096]{1,0:T(8,128)(2,1)}) custom-call(bf16[2,96,4096]{2,1,0:T(8,128)(2,1)} %bitcast.6, bf16[2,96,4096]{2,1,0:T(8,128)(2,1)} %bitcast.7, bf16[2,96,4096]{2,1,0:T(8,128)(2,1)} %bitcast.8, bf16[96,4096]{1,0:T(8,128)(2,1)} %bitcast.9, bf16[1,4096]{1,0:T(2,128)(2,1)} %gain.1, s32[1,1]{1,0:T(1,128)S(6)} %copy.11.steps, ...), custom_call_target="tpu_custom_call" | custom-call | tf_op jit(solution)/shard_map/pallas_call | solution.py:349
  71.7 0.0 copy-start
  71.7 2.1 %copy.13 = bf16[1,1,96,4096]{3,2,1,0:T(8,128)(2,1)} copy(bf16[1,1,96,4096]{3,2,1,0:T(8,128)(2,1)} %bitcast.11) | data formatting | bytes 1572864
  73.8 0.0 copy-done
  73.8 0.9 %copy.14 = bf16[1,1,96,4096]{3,2,1,0:T(8,128)(2,1)} copy(bf16[1,1,96,4096]{3,2,1,0:T(8,128)(2,1)S(1)} %bitcast.10) | data formatting | bytes 1572864
Async XLA Ops:
  71.7 2.1 %copy-start = (bf16[96,4096]{1,0:T(8,128)(2,1)S(1)}, bf16[96,4096]{1,0:T(8,128)(2,1)}, u32[]{:S(2)}) copy-start(bf16[96,4096]{1,0:T(8,128)(2,1)} %get-tuple-element.5) | copy-start | bytes 2359300

commit v2 on v1

--- a/solution.py
+++ b/solution.py
@@ -87,19 +87,34 @@
 MESH = pl.DeviceIdType.MESH
 HEADS_AT_ONCE = 4
 EARLY = 3
+LAG = 2
 TILE = 8
 LOG2E = 1.4426950408889634
 
 
-def partial_attention(query, key_rows, value_rows):
-    scores = lax.dot_general(
-        query, key_rows, (((1,), (1,)), ((), ())), preferred_element_type=jnp.float32
-    )
-    top = jnp.max(scores, axis=-1, keepdims=True)
-    powers = jnp.exp2((scores - top) * (HDIM ** (-0.5) * LOG2E))
-    total = jnp.sum(powers, axis=-1, keepdims=True)
-    part = jnp.dot(powers.astype(jnp.bfloat16), value_rows, preferred_element_type=jnp.float32)
-    return part, total, top * (HDIM ** (-0.5) * LOG2E) + jnp.log2(total)
+def partial_attentions(queries, key_blocks, value_blocks):
+    scores = [
+        lax.dot_general(query, rows, (((1,), (1,)), ((), ())), preferred_element_type=jnp.float32)
+        for query, rows in zip(queries, key_blocks)
+    ]
+    tops = [jnp.max(score, axis=-1, keepdims=True) for score in scores]
+    powers = [
+        jnp.exp2((score - top) * (HDIM ** (-0.5) * LOG2E)).astype(jnp.bfloat16)
+        for score, top in zip(scores, tops)
+    ]
+    ones = jnp.ones_like(value_blocks[0])
+    sums = [
+        jnp.dot(
+            power, jnp.concatenate([rows, ones], axis=1), preferred_element_type=jnp.float32
+        )
+        for power, rows in zip(powers, value_blocks)
+    ]
+    parts = [both[:, :HDIM] for both in sums]
+    totals = [both[:, HDIM:] for both in sums]
+    stats = [
+        top * (HDIM ** (-0.5) * LOG2E) + jnp.log2(total[:, :1]) for top, total in zip(tops, totals)
+    ]
+    return parts, totals, stats
 
 
 def share(mine, other):
@@ -121,37 +136,49 @@
 
 
 def pair_kernel(
-    queries, keys, values, latents, gain, steps, flags,
-    denoised, next_latents,
+    queries, keys, values, latents, gain_in, steps_in, flags_in,
+    denoised, lifted, base, scale_out,
     q_own, q_far, k_all, v_all, part_own, part_far, part_back, guided, guided_peer,
     now, now_peer, lse_own, lse_peer, lse_far, lse_back, squares, squares_peer,
-    gain_now, gain_move, gain_peer,
-    load_sems, kv_sems, q_sems, lse_sems, back_sems, stat_sems, cross_sems, ahead_sems,
+    gain, steps, flags, gain_now, gain_move, gain_peer, gain_next,
+    load_sems, kv_sems, q_sems, lse_sems, back_sems, stat_sems, cross_sems, ahead_sems, ready,
 ):
     seq = lax.axis_index("seq")
     size = lax.axis_size("seq")
-    beside = {"seq": seq + 1 - 2 * lax.rem(seq, 2)}
+    side = lax.rem(seq, 2)
+    beside = {"seq": seq + 1 - 2 * side}
     across = {"seq": lax.rem(seq + size // 2, size)}
     other = {"expert": 1 - lax.axis_index("expert")}
     branches, rows, width = queries.shape
     group = HEADS_AT_ONCE * HDIM
     groups = width // group
+    last = groups - 1
+
+    def signal(sem, peer):
+        pl.semaphore_signal(sem, inc=1, device_id=peer, device_id_type=MESH)
+
+    barrier = pltpu.get_barrier_semaphore()
+    signal(barrier, across)
+
+    @pl.when(side == 0)
+    def _():
+        signal(barrier, other)
+        signal(barrier, beside)
 
     own_keys = pl.ds(0, rows)
     peer_keys = pl.ds(rows, rows)
     loads = [
-        pltpu.make_async_copy(keys, k_all.at[:, own_keys], load_sems.at[0]),
-        pltpu.make_async_copy(queries, q_own, load_sems.at[1]),
-        pltpu.make_async_copy(values, v_all.at[:, own_keys], load_sems.at[2]),
-        pltpu.make_async_copy(latents, now, load_sems.at[3]),
+        pltpu.make_async_copy(steps_in, steps, load_sems.at[0]),
+        pltpu.make_async_copy(flags_in, flags, load_sems.at[1]),
+        pltpu.make_async_copy(gain_in, gain, load_sems.at[2]),
+        pltpu.make_async_copy(queries, q_own, load_sems.at[3]),
+        pltpu.make_async_copy(keys, k_all.at[:, own_keys], load_sems.at[4]),
+        pltpu.make_async_copy(values, v_all.at[:, own_keys], load_sems.at[5]),
+        pltpu.make_async_copy(latents, now, load_sems.at[6]),
     ]
     for load in loads:
         load.start()
-
-    barrier = pltpu.get_barrier_semaphore()
-    for peer in (beside, across, other):
-        pl.semaphore_signal(barrier, inc=1, device_id=peer, device_id_type=MESH)
-    pl.semaphore_wait(barrier, 3)
+    pl.semaphore_wait(barrier, 2)
 
     def remote(source, target, sems, index, peer):
         return pltpu.make_async_remote_copy(
@@ -179,33 +206,47 @@
     def lse_send(at):
         return remote(lse_own.at[at], lse_peer.at[at], lse_sems, at, across)
 
-    def back_sends(at):
-        cols = span(at)
-        return (
-            remote(lse_far.at[at], lse_back.at[at], stat_sems, at, across),
-            remote(part_far.at[:, cols], part_back.at[:, cols], back_sems, at, across),
-        )
-
-    def cross_send(at):
-        cols = span(at)
-        return remote(guided.at[:, cols], guided_peer.at[:, cols], cross_sems, at, other)
+    def stat_send(at):
+        return remote(lse_far.at[at], lse_back.at[at], stat_sems, at, across)
+
+    def back_send(cols, piece):
+        return remote(part_far.at[:, cols], part_back.at[:, cols], back_sems, piece, across)
+
+    def cross_send(cols, piece):
+        return remote(guided.at[:, cols], guided_peer.at[:, cols], cross_sems, piece, other)
+
+    endings = [(head_span(last, extra), last + extra) for extra in range(HEADS_AT_ONCE)]
 
     for at in range(min(EARLY, groups)):
         q_send(at).start()
 
-    def start_kv(at, carry):
-        for send in kv_sends(at):
-            send.start()
-        return carry
-
-    lax.fori_loop(0, groups, start_kv, 0)
+    def start_kv():
+        def step(at, carry):
+            for send in kv_sends(at):
+                send.start()
+            return carry
+
+        lax.fori_loop(0, groups, step, 0)
+
     ahead = [
         remote(latents, now_peer, ahead_sems, 0, other),
         remote(gain_move, gain_peer, ahead_sems, 1, other),
     ]
-    ahead[0].start()
-
-    step = jnp.full((1, HDIM), steps[0, 0], jnp.int32)
+
+    @pl.when(side == 0)
+    def _():
+        pl.semaphore_wait(ready.at[0], 1)
+        signal(ready.at[1], other)
+
+    @pl.when(side == 1)
+    def _():
+        signal(ready.at[0], beside)
+
+    start_kv()
+
+    for load in loads[:3]:
+        load.wait()
+    step = jnp.broadcast_to(steps[...], (1, HDIM))
     sigma_now = sigma_of(step)[:, :1]
     sigma_next = sigma_of(step + 1)[:, :1]
     row = gain[...].astype(jnp.float32)
@@ -213,22 +254,29 @@
     gain_move[...] = (sigma_next - sigma_now) * row
     squares[...] = jnp.zeros_like(squares)
     squares_peer[...] = jnp.zeros_like(squares_peer)
-
-    for load in loads:
+    for load in loads[3:]:
         load.wait()
+
+    def units_of(at):
+        return [
+            (branch, head_span(at, extra), extra * branches + branch)
+            for extra in range(HEADS_AT_ONCE)
+            for branch in range(branches)
+        ]
 
     def own_group(at, carry):
         for send in kv_sends(at):
             send.wait_recv()
+        units = units_of(at)
+        parts, totals, stats = partial_attentions(
+            [q_own[branch, :, cols] for branch, cols, _ in units],
+            [k_all[branch, :, cols] for branch, cols, _ in units],
+            [v_all[branch, :, cols] for branch, cols, _ in units],
+        )
         lse = jnp.zeros((TILE, HDIM), jnp.float32)
-        for extra in range(HEADS_AT_ONCE):
-            cols = head_span(at, extra)
-            for branch in range(branches):
-                part, total, stat = partial_attention(
-                    q_own[branch, :, cols], k_all[branch, :, cols], v_all[branch, :, cols]
-                )
-                part_own[branch, :, cols] = part / total
-                lse = pack(stat, extra * branches + branch, lse)
+        for (branch, cols, spot), part, total, stat in zip(units, parts, totals, stats):
+            part_own[branch, :, cols] = part / total
+            lse = pack(stat, spot, lse)
         lse_own[at] = lse
         lse_send(at).start()
 
@@ -239,52 +287,103 @@
         return carry
 
     lax.fori_loop(0, groups, own_group, 0)
-    ahead[1].start()
+
+    @pl.when(side == 0)
+    def _():
+        pl.semaphore_wait(ready.at[1], 1)
+        signal(ready.at[2], beside)
+
+    @pl.when(side == 1)
+    def _():
+        pl.semaphore_wait(ready.at[2], 1)
+
+    for send in ahead:
+        send.start()
 
     def far_group(at, carry):
         lse_send(at).wait_recv()
         q_send(at).wait_recv()
         theirs = lse_peer[at]
+        units = units_of(at)
+        parts, totals, stats = partial_attentions(
+            [q_far[branch, :, cols] for branch, cols, _ in units],
+            [k_all[branch, :, cols] for branch, cols, _ in units],
+            [v_all[branch, :, cols] for branch, cols, _ in units],
+        )
         lse = jnp.zeros((TILE, HDIM), jnp.float32)
+        terms = []
+        for (branch, cols, spot), part, total, stat in zip(units, parts, totals, stats):
+            lse = pack(stat, spot, lse)
+            factor = (GUIDANCE, 1.0 - GUIDANCE)[branch]
+            terms.append(part * (factor * share(stat, unpack(theirs, spot, rows)) / total))
         for extra in range(HEADS_AT_ONCE):
-            cols = head_span(at, extra)
-            terms = []
-            for branch, factor in ((0, GUIDANCE), (1, 1.0 - GUIDANCE)):
-                part, total, stat = partial_attention(
-                    q_far[branch, :, cols], k_all[branch, :, cols], v_all[branch, :, cols]
-                )
-                spot = extra * branches + branch
-                lse = pack(stat, spot, lse)
-                terms.append(part * (factor * share(stat, unpack(theirs, spot, rows)) / total))
-            part_far[:, cols] = (terms[0] + terms[1]).astype(jnp.bfloat16)
+            pair = terms[extra * branches] + terms[extra * branches + 1]
+            part_far[:, head_span(at, extra)] = pair.astype(jnp.bfloat16)
         lse_far[at] = lse
-        for send in back_sends(at):
-            send.start()
+        stat_send(at).start()
+
+        @pl.when(at < last)
+        def _():
+            back_send(span(at), at).start()
+
         return carry
 
     lax.fori_loop(0, groups, far_group, 0)
-
-    def add_squares(target, values_here):
-        target[...] += values_here * values_here
+    for cols, piece in endings:
+        back_send(cols, piece).start()
+
+    for send in ahead:
+        send.wait_recv()
+    trade_row = jnp.broadcast_to(flags[...], (1, width)) == 1
+    gain_next[...] = jnp.where(trade_row, gain_peer[...], gain_move[...])
+    trade = jnp.broadcast_to(flags[...], (rows, HDIM)) == 1
+
+    def finish_head(weight, cols, spot):
+        value = (
+            GUIDANCE * unpack(weight, spot, rows) * part_own[0, :, cols]
+            + (1.0 - GUIDANCE) * unpack(weight, spot + 1, rows) * part_own[1, :, cols]
+            + part_back[:, cols].astype(jnp.float32)
+        ).astype(jnp.bfloat16)
+        guided[:, cols] = value
+        wide = value.astype(jnp.float32)
+        squares[...] += wide * wide
+
+    def meet_head(cols):
+        theirs = guided_peer[:, cols].astype(jnp.float32)
+        squares_peer[...] += theirs * theirs
+        mine = guided[:, cols].astype(jnp.float32)
+        lifted[:, cols] = gain_next[:, cols] * jnp.where(trade, theirs, mine)
+        base[:, cols] = jnp.where(
+            trade, now_peer[:, cols].astype(jnp.float32), now[:, cols].astype(jnp.float32)
+        ).astype(jnp.bfloat16)
+
+    def meet_group(at):
+        cross_send(span(at), at).wait_recv()
+        for extra in range(HEADS_AT_ONCE):
+            meet_head(head_span(at, extra))
 
     def finish_group(at, carry):
-        for send in back_sends(at):
-            send.wait_recv()
+        stat_send(at).wait_recv()
+        back_send(span(at), at).wait_recv()
         weight = share(lse_own[at], lse_back[at])
         for extra in range(HEADS_AT_ONCE):
-            cols = head_span(at, extra)
-            spot = extra * branches
-            value = (
-                GUIDANCE * unpack(weight, spot, rows) * part_own[0, :, cols]
-                + (1.0 - GUIDANCE) * unpack(weight, spot + 1, rows) * part_own[1, :, cols]
-                + part_back[:, cols].astype(jnp.float32)
-            ).astype(jnp.bfloat16)
-            guided[:, cols] = value
-            add_squares(squares, value.astype(jnp.float32))
-        cross_send(at).start()
-        return carry
-
-    lax.fori_loop(0, groups, finish_group, 0)
+            finish_head(weight, head_span(at, extra), extra * branches)
+        cross_send(span(at), at).start()
+
+        @pl.when(at >= LAG)
+        def _():
+            meet_group(at - LAG)
+
+        return carry
+
+    lax.fori_loop(0, last, finish_group, 0)
+
+    stat_send(last).wait_recv()
+    weight = share(lse_own[last], lse_back[last])
+    for extra, (cols, piece) in enumerate(endings):
+        back_send(cols, piece).wait_recv()
+        finish_head(weight, cols, extra * branches)
+        cross_send(cols, piece).start()
 
     scale = lax.rsqrt(jnp.sum(squares[...], axis=-1, keepdims=True) / width + 1e-06)
 
@@ -299,58 +398,83 @@
 
     lax.fori_loop(0, groups, denoise_group, 0)
 
-    def peer_squares(at, carry):
-        cross_send(at).wait_recv()
-        for extra in range(HEADS_AT_ONCE):
-            add_squares(squares_peer, guided_peer[:, head_span(at, extra)].astype(jnp.float32))
-        return carry
-
-    lax.fori_loop(0, groups, peer_squares, 0)
+    def meet_rest(at, carry):
+        meet_group(at)
+        return carry
+
+    lax.fori_loop(max(last - LAG, 0), last, meet_rest, 0)
+    for cols, piece in endings:
+        cross_send(cols, piece).wait_recv()
+        meet_head(cols)
+    scale_peer = lax.rsqrt(jnp.sum(squares_peer[...], axis=-1, keepdims=True) / width + 1e-06)
+    scale_out[...] = jnp.where(trade, scale_peer, scale)
+
+    def drain(at, carry):
+        for send in (q_send(at), lse_send(at), stat_send(at)) + kv_sends(at):
+            send.wait_send()
+        return carry
+
+    def drain_pieces(at, carry):
+        for send in (back_send(span(at), at), cross_send(span(at), at)):
+            send.wait_send()
+        return carry
+
+    lax.fori_loop(0, groups, drain, 0)
+    lax.fori_loop(0, last, drain_pieces, 0)
+    for cols, piece in endings:
+        back_send(cols, piece).wait_send()
+        cross_send(cols, piece).wait_send()
     for send in ahead:
-        send.wait_recv()
-    scale_peer = lax.rsqrt(jnp.sum(squares_peer[...], axis=-1, keepdims=True) / width + 1e-06)
-    trade = jnp.full((rows, HDIM), flags[0], jnp.int32) == 1
+        send.wait_send()
+
+
+def place_kernel(denoised_in, lifted, base, scale, denoised, next_latents, rows_out, sems):
+    rows, width = base.shape
+    group = HEADS_AT_ONCE * HDIM
+    groups = width // group
+    whole = pltpu.make_async_copy(denoised_in, denoised, sems.at[groups])
+    whole.start()
+
+    def span(at):
+        return pl.ds(pl.multiple_of(at * group, group), group)
+
+    def store(at):
+        return pltpu.make_async_copy(rows_out.at[:, span(at)], next_latents.at[:, span(at)], sems.at[at])
 
     def move_group(at, carry):
         for extra in range(HEADS_AT_ONCE):
-            cols = head_span(at, extra)
-            mine = now[:, cols].astype(jnp.float32) + gain_move[:, cols] * (
-                guided[:, cols].astype(jnp.float32) * scale
-            )
-            theirs = now_peer[:, cols].astype(jnp.float32) + gain_peer[:, cols] * (
-                guided_peer[:, cols].astype(jnp.float32) * scale_peer
-            )
-            next_latents[:, cols] = jnp.where(trade, theirs, mine).astype(jnp.bfloat16)
+            cols = pl.ds(pl.multiple_of(at * group + extra * HDIM, HDIM), HDIM)
+            rows_out[:, cols] = (
+                base[:, cols].astype(jnp.float32) + lifted[:, cols] * scale[...]
+            ).astype(jnp.bfloat16)
+        store(at).start()
         return carry
 
     lax.fori_loop(0, groups, move_group, 0)
 
     def drain(at, carry):
-        for send in (q_send(at), lse_send(at), cross_send(at)) + kv_sends(at) + back_sends(at):
-            send.wait_send()
+        store(at).wait()
         return carry
 
     lax.fori_loop(0, groups, drain, 0)
-    for send in ahead:
-        send.wait_send()
+    whole.wait()
 
 
 def exchange_queries(queries, keys, values, latents, gain, steps_table, flags):
     branches, rows, width = queries.shape[2:]
     groups = width // (HEADS_AT_ONCE * HDIM)
-    whole = jax.ShapeDtypeStruct((rows, width), jnp.bfloat16)
-    hbm = pl.BlockSpec(memory_space=pltpu.HBM)
-    vmem = pl.BlockSpec(memory_space=pltpu.VMEM)
-    smem = pl.BlockSpec(memory_space=pltpu.SMEM)
+    pieces = groups - 1 + HEADS_AT_ONCE
     low = functools.partial(pltpu.VMEM, dtype=jnp.bfloat16)
     high = functools.partial(pltpu.VMEM, dtype=jnp.float32)
     dma = pltpu.SemaphoreType.DMA
+    hbm = pl.BlockSpec(memory_space=pltpu.HBM)
+    vmem = pl.BlockSpec(memory_space=pltpu.VMEM)
     stats = high((groups, TILE, HDIM))
-    denoised, next_latents = pl.pallas_call(
+    results = pl.pallas_call(
         pair_kernel,
-        out_shape=(whole, whole),
-        in_specs=[hbm] * 4 + [vmem, smem, smem],
-        out_specs=(vmem, vmem),
+        out_shape=(low((rows, width)), high((rows, width)), low((rows, width)), high((rows, HDIM))),
+        in_specs=[hbm] * 7,
+        out_specs=(vmem,) * 4,
         scratch_shapes=[
             low((branches, rows, width)),
             low((branches, rows, width)),
@@ -369,20 +493,36 @@
             stats,
             high((rows, HDIM)),
             high((rows, HDIM)),
+            low((1, width)),
+            pltpu.VMEM((1, 1), jnp.int32),
+            pltpu.VMEM((1, 1), jnp.int32),
             high((1, width)),
             high((1, width)),
             high((1, width)),
-            dma((4,)),
+            high((1, width)),
+            dma((7,)),
             dma((2, 2 * groups)),
             dma((2, groups)),
             dma((2, groups)),
+            dma((2, pieces)),
             dma((2, groups)),
-            dma((2, groups)),
-            dma((2, groups)),
+            dma((2, pieces)),
             dma((2, 2)),
+            pltpu.SemaphoreType.REGULAR((3,)),
         ],
         compiler_params=pltpu.CompilerParams(collective_id=0, has_side_effects=True),
-    )(queries[0, 0], keys[0, 0], values[0, 0], latents[0, 0], gain, steps_table, flags)
+    )(
+        queries[0, 0], keys[0, 0], values[0, 0], latents[0, 0], gain, steps_table,
+        flags.reshape(1, 1),
+    )
+    whole = jax.ShapeDtypeStruct((rows, width), jnp.bfloat16)
+    denoised, next_latents = pl.pallas_call(
+        place_kernel,
+        out_shape=(whole, whole),
+        in_specs=[vmem] * 4,
+        out_specs=(hbm, hbm),
+        scratch_shapes=[low((rows, width)), dma((groups + 1,))],
+    )(*(pltpu.with_memory_space_constraint(part, pltpu.VMEM) for part in results))
     return (denoised[None, None], next_latents[None, None])
 
 

time: 75 us -> 66.3 us (0.88)
  Pallas kernels: 69.8 us -> 64.2 us
  local copies, waits for them, and re-layouts: 3.02 us -> 0 us
    pallas_call x1 -> x2, Pallas kernels: 69.8 us -> 64.2 us  [the longest x1 63 us: exchange_queries(): pl.pallas_call(pair_kernel, out_shape=(low((rows, width)), high((rows, wi...]
    unnamed x4 -> x0, local copies, waits for them, and re-layouts: 3.02 us -> none
where the time goes in v2:
time: 66.3 us; the launch traced here: 66.1 us
  Pallas kernels  64.2 us (97%)
  between operations  1.93 us (3%)
    pallas_call x1, Pallas kernels, exchange_queries(): pl.pallas_call(pair_kernel, out_shape=(low((rows, width)), high((rows, wi...  63 us

profile of v2, /device:TPU:0, one launch (start us, length us, event | category | flops | bytes accessed | tf_op | source)
XLA Modules:
  0.0 66.1 jit_solution(7915504712303178186)
XLA Ops:
  1.9 63.0 %shard_map.86 = (bf16[96,4096]{1,0:T(8,128)(2,1)S(1)}, f32[96,4096]{1,0:T(8,128)S(1)}, bf16[96,4096]{1,0:T(8,128)(2,1)S(1)}, f32[96,128]{1,0:T(8,128)S(1)}) custom-call(bf16[2,96,4096]{2,1,0:T(8,128)(2,1)} %bitcast.8, bf16[2,96,4096]{2,1,0:T(8,128)(2,1)} %bitcast.9, bf16[2,96,4096]{2,1,0:T(8,128)(2,1)} %bitcast.10, bf16[96,4096]{1,0:T(8,128)(2,1)} %bitcast.11, ...), custom_call_target="tpu_custom_call" | custom-call | tf_op jit(solution)/shard_map/pallas_call | solution.py:473
  64.9 1.3 %shard_map.87 = (bf16[96,4096]{1,0:T(8,128)(2,1)}, bf16[96,4096]{1,0:T(8,128)(2,1)}) custom-call(bf16[96,4096]{1,0:T(8,128)(2,1)S(1)} %get-tuple-element.8.denoised_in, f32[96,4096]{1,0:T(8,128)S(1)} %get-tuple-element.9.lifted, bf16[96,4096]{1,0:T(8,128)(2,1)S(1)} %get-tuple-element.10.base, f32[96,128]{1,0:T(8,128)S(1)} %get-tuple-element.11.scale), custom_call_target="tpu_custom_call" | custom-call | tf_op jit(solution)/shard_map/pallas_call | solution.py:519

commit v3 on v2

--- a/solution.py
+++ b/solution.py
@@ -86,8 +86,11 @@
 
 MESH = pl.DeviceIdType.MESH
 HEADS_AT_ONCE = 4
-EARLY = 3
+AHEAD = 5
+FIRST = 2
+PIECE = 2
 LAG = 2
+MEET = AHEAD + LAG
 TILE = 8
 LOG2E = 1.4426950408889634
 
@@ -209,15 +212,26 @@
     def stat_send(at):
         return remote(lse_far.at[at], lse_back.at[at], stat_sems, at, across)
 
-    def back_send(cols, piece):
-        return remote(part_far.at[:, cols], part_back.at[:, cols], back_sems, piece, across)
-
-    def cross_send(cols, piece):
-        return remote(guided.at[:, cols], guided_peer.at[:, cols], cross_sems, piece, other)
-
-    endings = [(head_span(last, extra), last + extra) for extra in range(HEADS_AT_ONCE)]
-
-    for at in range(min(EARLY, groups)):
+    def back_send(first, many, piece):
+        heads = pl.ds(first, many)
+        return remote(part_far.at[heads], part_back.at[heads], back_sems, piece, across)
+
+    def cross_send(first, many, piece):
+        heads = pl.ds(first, many)
+        return remote(guided.at[heads], guided_peer.at[heads], cross_sems, piece, other)
+
+    cuts = HEADS_AT_ONCE // PIECE
+
+    def pieces_of(at):
+        return [
+            (at * HEADS_AT_ONCE + cut * PIECE, PIECE, at * cuts + cut) for cut in range(cuts)
+        ]
+
+    endings = [
+        (last * HEADS_AT_ONCE + extra, 1, last * cuts + extra) for extra in range(HEADS_AT_ONCE)
+    ]
+
+    for at in range(FIRST):
         q_send(at).start()
 
     def start_kv():
@@ -280,9 +294,9 @@
         lse_own[at] = lse
         lse_send(at).start()
 
-        @pl.when(at + EARLY < groups)
+        @pl.when(at < AHEAD - FIRST)
         def _():
-            q_send(at + EARLY).start()
+            q_send(at + FIRST).start()
 
         return carry
 
@@ -300,8 +314,9 @@
     for send in ahead:
         send.start()
 
-    def far_group(at, carry):
+    def far_group(at):
         lse_send(at).wait_recv()
+
         q_send(at).wait_recv()
         theirs = lse_peer[at]
         units = units_of(at)
@@ -318,79 +333,108 @@
             terms.append(part * (factor * share(stat, unpack(theirs, spot, rows)) / total))
         for extra in range(HEADS_AT_ONCE):
             pair = terms[extra * branches] + terms[extra * branches + 1]
-            part_far[:, head_span(at, extra)] = pair.astype(jnp.bfloat16)
+            part_far[at * HEADS_AT_ONCE + extra] = pair.astype(jnp.bfloat16)
         lse_far[at] = lse
         stat_send(at).start()
 
         @pl.when(at < last)
         def _():
-            back_send(span(at), at).start()
-
-        return carry
-
-    lax.fori_loop(0, groups, far_group, 0)
-    for cols, piece in endings:
-        back_send(cols, piece).start()
-
-    for send in ahead:
-        send.wait_recv()
-    trade_row = jnp.broadcast_to(flags[...], (1, width)) == 1
-    gain_next[...] = jnp.where(trade_row, gain_peer[...], gain_move[...])
+            for piece in pieces_of(at):
+                back_send(*piece).start()
+
+        @pl.when(at + AHEAD < groups)
+        def _():
+            q_send(at + AHEAD).start()
+
     trade = jnp.broadcast_to(flags[...], (rows, HDIM)) == 1
 
-    def finish_head(weight, cols, spot):
-        value = (
+    def own_term(weight, at, extra):
+        cols = head_span(at, extra)
+        spot = extra * branches
+        return (
             GUIDANCE * unpack(weight, spot, rows) * part_own[0, :, cols]
             + (1.0 - GUIDANCE) * unpack(weight, spot + 1, rows) * part_own[1, :, cols]
-            + part_back[:, cols].astype(jnp.float32)
-        ).astype(jnp.bfloat16)
-        guided[:, cols] = value
+        )
+
+    def finish_head(term, head):
+        value = (term + part_back[head].astype(jnp.float32)).astype(jnp.bfloat16)
+        guided[head] = value
         wide = value.astype(jnp.float32)
         squares[...] += wide * wide
 
-    def meet_head(cols):
-        theirs = guided_peer[:, cols].astype(jnp.float32)
+    def meet_head(at, extra):
+        cols = head_span(at, extra)
+        head = at * HEADS_AT_ONCE + extra
+        theirs = guided_peer[head].astype(jnp.float32)
         squares_peer[...] += theirs * theirs
-        mine = guided[:, cols].astype(jnp.float32)
+        mine = guided[head].astype(jnp.float32)
         lifted[:, cols] = gain_next[:, cols] * jnp.where(trade, theirs, mine)
         base[:, cols] = jnp.where(
             trade, now_peer[:, cols].astype(jnp.float32), now[:, cols].astype(jnp.float32)
         ).astype(jnp.bfloat16)
 
     def meet_group(at):
-        cross_send(span(at), at).wait_recv()
+        for piece in pieces_of(at):
+            cross_send(*piece).wait_recv()
         for extra in range(HEADS_AT_ONCE):
-            meet_head(head_span(at, extra))
-
-    def finish_group(at, carry):
+            meet_head(at, extra)
+
+    def finish_group(at):
         stat_send(at).wait_recv()
-        back_send(span(at), at).wait_recv()
         weight = share(lse_own[at], lse_back[at])
-        for extra in range(HEADS_AT_ONCE):
-            finish_head(weight, head_span(at, extra), extra * branches)
-        cross_send(span(at), at).start()
-
-        @pl.when(at >= LAG)
+        terms = [own_term(weight, at, extra) for extra in range(HEADS_AT_ONCE)]
+        for cut, piece in enumerate(pieces_of(at)):
+            back_send(*piece).wait_recv()
+            for extra in range(cut * PIECE, (cut + 1) * PIECE):
+                finish_head(terms[extra], at * HEADS_AT_ONCE + extra)
+            cross_send(*piece).start()
+
+    def step_group(at, carry):
+        @pl.when(at >= AHEAD)
         def _():
-            meet_group(at - LAG)
-
-        return carry
-
-    lax.fori_loop(0, last, finish_group, 0)
+            finish_group(at - AHEAD)
+
+        far_group(at)
+
+        @pl.when(at == MEET)
+        def _():
+            for send in ahead:
+                send.wait_recv()
+            trade_row = jnp.broadcast_to(flags[...], (1, width)) == 1
+            gain_next[...] = jnp.where(trade_row, gain_peer[...], gain_move[...])
+
+        @pl.when(at >= MEET)
+        def _():
+            meet_group(at - MEET)
+
+        return carry
+
+    lax.fori_loop(0, groups, step_group, 0)
+    for piece in endings:
+        back_send(*piece).start()
+
+    def late_group(at, carry):
+        finish_group(at)
+        meet_group(at - LAG)
+        return carry
+
+    lax.fori_loop(groups - AHEAD, last, late_group, 0)
 
     stat_send(last).wait_recv()
     weight = share(lse_own[last], lse_back[last])
-    for extra, (cols, piece) in enumerate(endings):
-        back_send(cols, piece).wait_recv()
-        finish_head(weight, cols, extra * branches)
-        cross_send(cols, piece).start()
+    for extra in range(HEADS_AT_ONCE):
+        part_own[0, :, head_span(last, extra)] = own_term(weight, last, extra)
+    for extra, piece in enumerate(endings):
+        back_send(*piece).wait_recv()
+        finish_head(part_own[0, :, head_span(last, extra)], piece[0])
+        cross_send(*piece).start()
 
     scale = lax.rsqrt(jnp.sum(squares[...], axis=-1, keepdims=True) / width + 1e-06)
 
     def denoise_group(at, carry):
         for extra in range(HEADS_AT_ONCE):
             cols = head_span(at, extra)
-            unit = guided[:, cols].astype(jnp.float32) * scale
+            unit = guided[at * HEADS_AT_ONCE + extra].astype(jnp.float32) * scale
             denoised[:, cols] = (
                 now[:, cols].astype(jnp.float32) - gain_now[:, cols] * unit
             ).astype(jnp.bfloat16)
@@ -398,34 +442,37 @@
 
     lax.fori_loop(0, groups, denoise_group, 0)
 
-    def meet_rest(at, carry):
+    def drain(at, carry):
+        for send in (lse_send(at), stat_send(at)) + kv_sends(at):
+            send.wait_send()
+        return carry
+
+    def drain_groups(at, carry):
+        for piece in pieces_of(at):
+            back_send(*piece).wait_send()
+            cross_send(*piece).wait_send()
+        return carry
+
+    def drain_queries(at, carry):
+        q_send(at).wait_send()
+        return carry
+
+    lax.fori_loop(0, groups, drain, 0)
+    lax.fori_loop(0, last, drain_groups, 0)
+    lax.fori_loop(0, groups, drain_queries, 0)
+    for send in ahead:
+        send.wait_send()
+    for piece in endings:
+        back_send(*piece).wait_send()
+    for at in range(last - LAG, last):
         meet_group(at)
-        return carry
-
-    lax.fori_loop(max(last - LAG, 0), last, meet_rest, 0)
-    for cols, piece in endings:
-        cross_send(cols, piece).wait_recv()
-        meet_head(cols)
+    for extra, piece in enumerate(endings):
+        cross_send(*piece).wait_recv()
+        meet_head(last, extra)
     scale_peer = lax.rsqrt(jnp.sum(squares_peer[...], axis=-1, keepdims=True) / width + 1e-06)
     scale_out[...] = jnp.where(trade, scale_peer, scale)
-
-    def drain(at, carry):
-        for send in (q_send(at), lse_send(at), stat_send(at)) + kv_sends(at):
-            send.wait_send()
-        return carry
-
-    def drain_pieces(at, carry):
-        for send in (back_send(span(at), at), cross_send(span(at), at)):
-            send.wait_send()
-        return carry
-
-    lax.fori_loop(0, groups, drain, 0)
-    lax.fori_loop(0, last, drain_pieces, 0)
-    for cols, piece in endings:
-        back_send(cols, piece).wait_send()
-        cross_send(cols, piece).wait_send()
-    for send in ahead:
-        send.wait_send()
+    for piece in endings:
+        cross_send(*piece).wait_send()
 
 
 def place_kernel(denoised_in, lifted, base, scale, denoised, next_latents, rows_out, sems):
@@ -435,41 +482,33 @@
     whole = pltpu.make_async_copy(denoised_in, denoised, sems.at[groups])
     whole.start()
 
-    def span(at):
-        return pl.ds(pl.multiple_of(at * group, group), group)
-
-    def store(at):
-        return pltpu.make_async_copy(rows_out.at[:, span(at)], next_latents.at[:, span(at)], sems.at[at])
-
-    def move_group(at, carry):
+    stores = [whole]
+    for at in range(groups):
         for extra in range(HEADS_AT_ONCE):
-            cols = pl.ds(pl.multiple_of(at * group + extra * HDIM, HDIM), HDIM)
+            cols = pl.ds(at * group + extra * HDIM, HDIM)
             rows_out[:, cols] = (
                 base[:, cols].astype(jnp.float32) + lifted[:, cols] * scale[...]
             ).astype(jnp.bfloat16)
-        store(at).start()
-        return carry
-
-    lax.fori_loop(0, groups, move_group, 0)
-
-    def drain(at, carry):
-        store(at).wait()
-        return carry
-
-    lax.fori_loop(0, groups, drain, 0)
-    whole.wait()
+        here = pl.ds(at * group, group)
+        stores.append(
+            pltpu.make_async_copy(rows_out.at[:, here], next_latents.at[:, here], sems.at[at])
+        )
+        stores[-1].start()
+    for store in stores:
+        store.wait()
 
 
 def exchange_queries(queries, keys, values, latents, gain, steps_table, flags):
     branches, rows, width = queries.shape[2:]
     groups = width // (HEADS_AT_ONCE * HDIM)
-    pieces = groups - 1 + HEADS_AT_ONCE
+    pieces = (groups - 1) * (HEADS_AT_ONCE // PIECE) + HEADS_AT_ONCE
     low = functools.partial(pltpu.VMEM, dtype=jnp.bfloat16)
     high = functools.partial(pltpu.VMEM, dtype=jnp.float32)
     dma = pltpu.SemaphoreType.DMA
     hbm = pl.BlockSpec(memory_space=pltpu.HBM)
     vmem = pl.BlockSpec(memory_space=pltpu.VMEM)
     stats = high((groups, TILE, HDIM))
+    by_head = low((width // HDIM, rows, HDIM))
     results = pl.pallas_call(
         pair_kernel,
         out_shape=(low((rows, width)), high((rows, width)), low((rows, width)), high((rows, HDIM))),
@@ -481,10 +520,10 @@
             low((branches, 2 * rows, width)),
             low((branches, 2 * rows, width)),
             high((branches, rows, width)),
-            low((rows, width)),
-            low((rows, width)),
-            low((rows, width)),
-            low((rows, width)),
+            by_head,
+            by_head,
+            by_head,
+            by_head,
             low((rows, width)),
             low((rows, width)),
             stats,
@@ -536,6 +575,7 @@
         and rows // TILE * HEADS_AT_ONCE * branches <= HDIM
         and HEADS_AT_ONCE * branches <= TILE
         and width % (HEADS_AT_ONCE * HDIM) == 0
+        and width // (HEADS_AT_ONCE * HDIM) > MEET
     )
     return (exchange_queries if paired else exchange_heads)(*blocks)
 

time: 66.3 us -> 65.1 us (0.982)
  Pallas kernels: 64.2 us -> 63 us
    pallas_call x1, Pallas kernels: 63 us -> 61.8 us  [exchange_queries(): pl.pallas_call(pair_kernel, out_shape=(low((rows, width)), high((rows, wi...]
where the time goes in v3:
time: 65.1 us; the launch traced here: 64.9 us
  Pallas kernels  63 us (97%)
  between operations  1.93 us (3%)
    pallas_call x1, Pallas kernels, exchange_queries(): pl.pallas_call(pair_kernel, out_shape=(low((rows, width)), high((rows, wi...  61.8 us

profile of v3, /device:TPU:0, one launch (start us, length us, event | category | flops | bytes accessed | tf_op | source)
XLA Modules:
  0.0 64.9 jit_solution(13271133790478259573)
XLA Ops:
  1.9 61.8 %shard_map.86 = (bf16[96,4096]{1,0:T(8,128)(2,1)S(1)}, f32[96,4096]{1,0:T(8,128)S(1)}, bf16[96,4096]{1,0:T(8,128)(2,1)S(1)}, f32[96,128]{1,0:T(8,128)S(1)}) custom-call(bf16[2,96,4096]{2,1,0:T(8,128)(2,1)} %bitcast.8, bf16[2,96,4096]{2,1,0:T(8,128)(2,1)} %bitcast.9, bf16[2,96,4096]{2,1,0:T(8,128)(2,1)} %bitcast.10, bf16[96,4096]{1,0:T(8,128)(2,1)} %bitcast.11, ...), custom_call_target="tpu_custom_call" | custom-call | tf_op jit(solution)/shard_map/pallas_call | solution.py:512
  63.7 1.2 %shard_map.87 = (bf16[96,4096]{1,0:T(8,128)(2,1)}, bf16[96,4096]{1,0:T(8,128)(2,1)}) custom-call(bf16[96,4096]{1,0:T(8,128)(2,1)S(1)} %get-tuple-element.8.denoised_in, f32[96,4096]{1,0:T(8,128)S(1)} %get-tuple-element.9.lifted, bf16[96,4096]{1,0:T(8,128)(2,1)S(1)} %get-tuple-element.10.base, f32[96,128]{1,0:T(8,128)S(1)} %get-tuple-element.11.scale), custom_call_target="tpu_custom_call" | custom-call | tf_op jit(solution)/shard_map/pallas_call | solution.py:558

commit v4 on v3

--- a/solution.py
+++ b/solution.py
@@ -86,9 +86,9 @@
 
 MESH = pl.DeviceIdType.MESH
 HEADS_AT_ONCE = 4
-AHEAD = 5
+AHEAD = 4
 FIRST = 2
-PIECE = 2
+PIECE = 4
 LAG = 2
 MEET = AHEAD + LAG
 TILE = 8
@@ -142,7 +142,7 @@
     queries, keys, values, latents, gain_in, steps_in, flags_in,
     denoised, lifted, base, scale_out,
     q_own, q_far, k_all, v_all, part_own, part_far, part_back, guided, guided_peer,
-    now, now_peer, lse_own, lse_peer, lse_far, lse_back, squares, squares_peer,
+    now, now_peer, lse_own, lse_peer, keep_far, keep_back, squares, squares_peer,
     gain, steps, flags, gain_now, gain_move, gain_peer, gain_next,
     load_sems, kv_sems, q_sems, lse_sems, back_sems, stat_sems, cross_sems, ahead_sems, ready,
 ):
@@ -210,7 +210,7 @@
         return remote(lse_own.at[at], lse_peer.at[at], lse_sems, at, across)
 
     def stat_send(at):
-        return remote(lse_far.at[at], lse_back.at[at], stat_sems, at, across)
+        return remote(keep_far.at[at], keep_back.at[at], stat_sems, at, across)
 
     def back_send(first, many, piece):
         heads = pl.ds(first, many)
@@ -227,9 +227,13 @@
             (at * HEADS_AT_ONCE + cut * PIECE, PIECE, at * cuts + cut) for cut in range(cuts)
         ]
 
-    endings = [
-        (last * HEADS_AT_ONCE + extra, 1, last * cuts + extra) for extra in range(HEADS_AT_ONCE)
-    ]
+    late = groups - AHEAD
+
+    def singles_of(at):
+        return [
+            (at * HEADS_AT_ONCE + extra, 1, late * cuts + (at - late) * HEADS_AT_ONCE + extra)
+            for extra in range(HEADS_AT_ONCE)
+        ]
 
     for at in range(FIRST):
         q_send(at).start()
@@ -334,12 +338,17 @@
         for extra in range(HEADS_AT_ONCE):
             pair = terms[extra * branches] + terms[extra * branches + 1]
             part_far[at * HEADS_AT_ONCE + extra] = pair.astype(jnp.bfloat16)
-        lse_far[at] = lse
+        keep_far[at] = share(theirs, lse).astype(jnp.bfloat16)
         stat_send(at).start()
 
-        @pl.when(at < last)
+        @pl.when(at < late)
         def _():
             for piece in pieces_of(at):
+                back_send(*piece).start()
+
+        @pl.when(at >= late)
+        def _():
+            for piece in singles_of(at):
                 back_send(*piece).start()
 
         @pl.when(at + AHEAD < groups)
@@ -373,26 +382,27 @@
             trade, now_peer[:, cols].astype(jnp.float32), now[:, cols].astype(jnp.float32)
         ).astype(jnp.bfloat16)
 
-    def meet_group(at):
-        for piece in pieces_of(at):
+    def meet_group(at, pieces):
+        for piece in pieces:
             cross_send(*piece).wait_recv()
         for extra in range(HEADS_AT_ONCE):
             meet_head(at, extra)
 
-    def finish_group(at):
+    def finish_group(at, pieces):
         stat_send(at).wait_recv()
-        weight = share(lse_own[at], lse_back[at])
+        weight = keep_back[at].astype(jnp.float32)
         terms = [own_term(weight, at, extra) for extra in range(HEADS_AT_ONCE)]
-        for cut, piece in enumerate(pieces_of(at)):
+        for piece in pieces:
             back_send(*piece).wait_recv()
-            for extra in range(cut * PIECE, (cut + 1) * PIECE):
-                finish_head(terms[extra], at * HEADS_AT_ONCE + extra)
+            many = piece[1]
+            for extra in range(many):
+                finish_head(terms.pop(0), piece[0] + extra)
             cross_send(*piece).start()
 
     def step_group(at, carry):
         @pl.when(at >= AHEAD)
         def _():
-            finish_group(at - AHEAD)
+            finish_group(at - AHEAD, pieces_of(at - AHEAD))
 
         far_group(at)
 
@@ -405,29 +415,26 @@
 
         @pl.when(at >= MEET)
         def _():
-            meet_group(at - MEET)
+            meet_group(at - MEET, pieces_of(at - MEET))
 
         return carry
 
     lax.fori_loop(0, groups, step_group, 0)
-    for piece in endings:
-        back_send(*piece).start()
-
     def late_group(at, carry):
-        finish_group(at)
-        meet_group(at - LAG)
-        return carry
-
-    lax.fori_loop(groups - AHEAD, last, late_group, 0)
-
-    stat_send(last).wait_recv()
-    weight = share(lse_own[last], lse_back[last])
-    for extra in range(HEADS_AT_ONCE):
-        part_own[0, :, head_span(last, extra)] = own_term(weight, last, extra)
-    for extra, piece in enumerate(endings):
-        back_send(*piece).wait_recv()
-        finish_head(part_own[0, :, head_span(last, extra)], piece[0])
-        cross_send(*piece).start()
+        finish_group(at, singles_of(at))
+
+        @pl.when(at - LAG < late)
+        def _():
+            meet_group(at - LAG, pieces_of(at - LAG))
+
+        @pl.when(at - LAG >= late)
+        def _():
+            meet_group(at - LAG, singles_of(at - LAG))
+
+        return carry
+
+    lax.fori_loop(late, last, late_group, 0)
+    finish_group(last, singles_of(last))
 
     scale = lax.rsqrt(jnp.sum(squares[...], axis=-1, keepdims=True) / width + 1e-06)
 
@@ -453,25 +460,32 @@
             cross_send(*piece).wait_send()
         return carry
 
+    def drain_late(at, carry):
+        for piece in singles_of(at):
+            back_send(*piece).wait_send()
+            cross_send(*piece).wait_send()
+        return carry
+
     def drain_queries(at, carry):
         q_send(at).wait_send()
         return carry
 
     lax.fori_loop(0, groups, drain, 0)
-    lax.fori_loop(0, last, drain_groups, 0)
+    lax.fori_loop(0, late, drain_groups, 0)
+    lax.fori_loop(late, last, drain_late, 0)
     lax.fori_loop(0, groups, drain_queries, 0)
     for send in ahead:
         send.wait_send()
-    for piece in endings:
+    for piece in singles_of(last):
         back_send(*piece).wait_send()
     for at in range(last - LAG, last):
-        meet_group(at)
-    for extra, piece in enumerate(endings):
+        meet_group(at, singles_of(at) if at >= late else pieces_of(at))
+    for extra, piece in enumerate(singles_of(last)):
         cross_send(*piece).wait_recv()
         meet_head(last, extra)
     scale_peer = lax.rsqrt(jnp.sum(squares_peer[...], axis=-1, keepdims=True) / width + 1e-06)
     scale_out[...] = jnp.where(trade, scale_peer, scale)
-    for piece in endings:
+    for piece in singles_of(last):
         cross_send(*piece).wait_send()
 
 
@@ -501,7 +515,7 @@
 def exchange_queries(queries, keys, values, latents, gain, steps_table, flags):
     branches, rows, width = queries.shape[2:]
     groups = width // (HEADS_AT_ONCE * HDIM)
-    pieces = (groups - 1) * (HEADS_AT_ONCE // PIECE) + HEADS_AT_ONCE
+    pieces = (groups - AHEAD) * (HEADS_AT_ONCE // PIECE) + AHEAD * HEADS_AT_ONCE
     low = functools.partial(pltpu.VMEM, dtype=jnp.bfloat16)
     high = functools.partial(pltpu.VMEM, dtype=jnp.float32)
     dma = pltpu.SemaphoreType.DMA
@@ -528,8 +542,8 @@
             low((rows, width)),
             stats,
             stats,
-            stats,
-            stats,
+            low((groups, TILE, HDIM)),
+            low((groups, TILE, HDIM)),
             high((rows, HDIM)),
             high((rows, HDIM)),
             low((1, width)),

time: 65.1 us -> 64.7 us (level)
  no operation moved by 1% of the time
where the time goes in v4:
time: 64.7 us; the launch traced here: 64.6 us
  Pallas kernels  62.6 us (97%)
  between operations  1.93 us (3%)
    pallas_call x1, Pallas kernels, exchange_queries(): pl.pallas_call(pair_kernel, out_shape=(low((rows, width)), high((rows, wi...  61.4 us

profile of v4, /device:TPU:0, one launch (start us, length us, event | category | flops | bytes accessed | tf_op | source)
XLA Modules:
  0.0 64.6 jit_solution(8159438494245683886)
XLA Ops:
  1.9 61.4 %shard_map.86 = (bf16[96,4096]{1,0:T(8,128)(2,1)S(1)}, f32[96,4096]{1,0:T(8,128)S(1)}, bf16[96,4096]{1,0:T(8,128)(2,1)S(1)}, f32[96,128]{1,0:T(8,128)S(1)}) custom-call(bf16[2,96,4096]{2,1,0:T(8,128)(2,1)} %bitcast.8, bf16[2,96,4096]{2,1,0:T(8,128)(2,1)} %bitcast.9, bf16[2,96,4096]{2,1,0:T(8,128)(2,1)} %bitcast.10, bf16[96,4096]{1,0:T(8,128)(2,1)} %bitcast.11, ...), custom_call_target="tpu_custom_call" | custom-call | tf_op jit(solution)/shard_map/pallas_call | solution.py:526
  63.4 1.2 %shard_map.87 = (bf16[96,4096]{1,0:T(8,128)(2,1)}, bf16[96,4096]{1,0:T(8,128)(2,1)}) custom-call(bf16[96,4096]{1,0:T(8,128)(2,1)S(1)} %get-tuple-element.8.denoised_in, f32[96,4096]{1,0:T(8,128)S(1)} %get-tuple-element.9.lifted, bf16[96,4096]{1,0:T(8,128)(2,1)S(1)} %get-tuple-element.10.base, f32[96,128]{1,0:T(8,128)S(1)} %get-tuple-element.11.scale), custom_call_target="tpu_custom_call" | custom-call | tf_op jit(solution)/shard_map/pallas_call | solution.py:572
